TPU v7x, 32 devices: a whole 2x2x4 slice. The times are simulated.
32 devices in a mesh: row: 4 (over y, x), col: 8 (over z, core).
Axes of the slice: x: 2, y: 2, z: 4, core: 2. Of those that a mesh axis runs over, the one named last changes fastest.
Arguments:
- left_tiles: bfloat16 [2, 32, 256, 256], P(None, 'row', 'col'), may hold values from 0.02 to 3, as said below
- right_tile_store: bfloat16 [32, 24, 256, 256], P('col', 'row'), may hold values from 0.019897461 to 1
- right_index: int32 [32, 24], P('col', 'row'), may hold values from 0 to 7, as said below
- right_count: int32 [32, 4], P('col', 'row'), may hold values from 1 to 6
Outputs:
- inflated: bfloat16 [2, 32, 256, 256], P(None, 'col', 'row')
Inputs may be any that keep to these rules, and one draw needn't show every extreme that they name: `right_index`: for each column block and each row index the 6 slots name distinct contraction blocks; only the first right_count of them are used. `left_tiles`: positive entries.
All inputs are finite; a program needn't handle non-finite values.
Results may differ from a plain program's by a relative error of at most 0.001.
Values may be sent and summed in bfloat16 or wider, within the bound.
No kernel may reach another device: no remote copies, remote signals or barrier semaphores. Data moves between devices by JAX's collectives and lax.ppermute only.
A program may use at most 64 MiB of HBM per device.

v0:
```python
import jax
import jax.numpy as jnp
from jax import lax
from jax.sharding import PartitionSpec as P


def shards(left_tiles, right_tile_store, right_index, right_count):
    column_blocks = right_tile_store.shape[0]
    slot_total = right_tile_store.shape[1]
    window_blocks = left_tiles.shape[0]
    tile_size = right_tile_store.shape[2]
    live_mask = (jnp.arange(slot_total, dtype=jnp.int32)[None, :] < right_count).astype(
        jnp.bfloat16
    )
    flat_index = right_index.reshape(-1)
    shard_rows = lax.all_gather(left_tiles, "col", axis=2, tiled=True)
    picked = jnp.take(shard_rows, flat_index, axis=1)
    picked = picked.reshape(
        window_blocks, column_blocks, slot_total, shard_rows.shape[2], shard_rows.shape[3]
    )
    picked = picked * live_mask[None, :, :, None, None]
    partial_value = jnp.einsum(
        "ajqmb,jqbn->ajmn", picked, right_tile_store, preferred_element_type=jnp.float32
    )
    share = lax.psum_scatter(partial_value, "row", scatter_dimension=2, tiled=True)
    squared = share * share
    column_sums = lax.psum(jnp.sum(squared, axis=(0, 2)), "row")
    scaled = squared * (window_blocks * tile_size / column_sums[None, :, None, :])
    return scaled.astype(jnp.bfloat16)


def solution(mesh):
    in_specs = (
        P(None, "row", "col", None),
        P("col", "row", None, None),
        P("col", "row"),
        P("col", "row"),
    )
    out_specs = P(None, "col", "row", None)
    return jax.shard_map(shards, mesh=mesh, in_specs=in_specs, out_specs=out_specs, check_vma=False)
```

profile of v0, /device:TPU:0, one launch (start us, length us, event | category | flops | bytes accessed | tf_op | source)
XLA Modules:
  0.0 106.3 jit_solution(15490569830004205076)
XLA Ops:
  6.5 0.0 copy-start
  6.5 0.0 all-gather.2.cloned.1.call-start
  6.5 0.7 all-gather.2.cloned.1.call-update
  7.3 0.0 reduce-scatter.2.cloned.1.call-start
  7.3 0.9 reshape.66
  8.3 0.8 fusion.12
  9.0 31.8 %all-gather.2.cloned.1.call-done = bf16[2,8,256,256]{3,2,1,0:T(8,128)(2,1)} async-done(((bf16[2,8,32,256]{3,2,1,0:T(8,128)(2,1)}), bf16[2,8,256,256]{3,2,1,0:T(8,128)(2,1)}) %all-gather.2.cloned.1.call-update) | async-done | bytes 2097168 | tf_op jit(solution)/shard_map/all_gather | solution.py:16
  40.8 6.0 %gather_fusion = bf16[24,2,256,256]{3,2,1,0:T(8,128)(2,1)} fusion(bf16[2,8,256,256]{3,2,1,0:T(8,128)(2,1)} %all-gather.2.cloned.1.call-done, s32[1024]{0:T(1024)S(1)} %pad_clamp_fusion), kind=kCustom, calls=%fused_computation | custom fusion | bytes 12583008 | tf_op jit(solution)/shard_map/jit(_take)/gather | solution.py:17
  46.8 0.0 copy-done
  46.8 6.0 %fusion.7 = f32[2,4,256,256]{3,2,0,1:T(8,128)} fusion(bf16[4,6,256,256]{3,2,1,0:T(8,128)(2,1)S(1)} %copy-done, bf16[2,4,6,256,256]{4,3,0,2,1:T(8,128)(2,1)} %bitcast.18, pred[4,6]{1,0:T(4,128)(4,1)S(1)} %get-tuple-element.6, bf16[4,6]{1,0:T(4,128)(2,1)S(1)} %get-tuple-element.5), kind=kOutput, calls=%fused_computation.8 | convolution fusion | flops 1616904192 | bytes 11534408 | tf_op jit(solution)/shard_map/ajqmb,jqbn->ajmn/dot_general | solution.py:22
  52.8 0.0 reduce-scatter.2.cloned.1.call-update
  52.8 34.7 %reduce-scatter.2.cloned.1.call-done = f32[2,4,64,256]{3,2,0,1:T(8,128)} async-done(((f32[2,4,256,256]{3,2,0,1:T(8,128)}), f32[2,4,64,256]{3,2,0,1:T(8,128)}) %reduce-scatter.2.cloned.1.call-update) | async-done | bytes 524304 | tf_op jit(solution)/shard_map/reduce_scatter | solution.py:25
  87.6 1.1 %multiply_reduce_fusion = f32[4,256]{1,0:T(4,128)S(1)} fusion(f32[2,4,64,256]{3,2,0,1:T(8,128)} %reduce-scatter.2.cloned.1.call-done), kind=kLoop, calls=%fused_computation.10 | loop fusion | flops 261120 | bytes 528384 | tf_op jit(solution)/shard_map/reduce_sum | solution.py:27
  88.7 9.0 %psum.7 = f32[4,256]{1,0:T(4,128)S(1)} all-reduce(f32[4,256]{1,0:T(4,128)S(1)} %multiply_reduce_fusion), channel_id=1, replica_groups=mesh['row'=4,'col'=8] {'row'}, use_global_device_ids=true, to_apply=%region_2.3 | all-reduce | flops 1024 | bytes 8192 | tf_op jit(solution)/shard_map/psum | solution.py:27
  97.6 1.1 %multiply_convert_fusion = bf16[2,4,64,256]{3,2,0,1:T(8,128)(2,1)S(1)} fusion(f32[2,4,64,256]{3,2,0,1:T(8,128)} %reduce-scatter.2.cloned.1.call-done, f32[4,256]{1,0:T(4,128)S(1)} %broadcast_divide_fusion), kind=kLoop, calls=%fused_computation.9 | loop fusion | flops 393216 | bytes 790528 | tf_op jit(solution)/shard_map/convert_element_type | solution.py:29
  98.7 0.7 copy.6
  (3 shorter events, 0.0 us)
Async XLA Ops:
  6.5 40.3 %copy-start = (bf16[4,6,256,256]{3,2,1,0:T(8,128)(2,1)S(1)}, bf16[4,6,256,256]{3,2,1,0:T(8,128)(2,1)}, u32[]{:S(2)}) copy-start(bf16[4,6,256,256]{3,2,1,0:T(8,128)(2,1)} %param.5) | copy-start | bytes 9437188
  6.5 34.3 %all-gather.2.cloned.1.call-start = ((), (), s32[]{:S(2)}) async-start(), calls=%async_computation.1 | async-start | bytes 2359296 | tf_op jit(solution)/shard_map/all_gather | solution.py:16
  7.3 80.3 %reduce-scatter.2.cloned.1.call-start = ((), (), s32[]{:S(2)}) async-start(), calls=%async_computation.2 | async-start | bytes 2621440 | tf_op jit(solution)/shard_map/reduce_scatter | solution.py:25
Sparse Core Ops, SparseCore 0:
  8.9 31.8 all-gather.1
  52.9 34.5 reduce-scatter.1
where the time goes:
time: 107 us; the launch traced here: 106 us
  waiting for transfers between devices  67.3 us (63%)
  between operations  13.4 us (13%)
  blocking collectives  8.97 us (8%)
  local copies, waits for them, and re-layouts  7.65 us (7%)
  matrix products  5.96 us (6%)
  other arithmetic  2.98 us (3%)
    reduce_scatter x1, waiting for transfers between devices, shards(): lax.psum_scatter(partial_value, 'row', scatter_dimension=2, tiled=True)  34.7 us
    all_gather x1, waiting for transfers between devices, shards(): shard_rows = lax.all_gather(left_tiles, 'col', axis=2, tiled=True)  31.8 us
    psum x1, blocking collectives, shards(): column_sums = lax.psum(jnp.sum(squared, axis=(0, 2)), 'row')  8.97 us
    gather x1, local copies, waits for them, and re-layouts, shards(): picked = jnp.take(shard_rows, flat_index, axis=1)  5.99 us
    dot_general x1, matrix products, shards(): jnp.einsum('ajqmb,jqbn->ajmn', picked, right_tile_store, preferred_elemen...  5.96 us
  transfers between devices with their start and end apart: 2, of which 2 were waited for; matrix products, arithmetic and copies ran while one was open for 2% of the time, Pallas kernels for 0%

commit v1 on v0

--- a/solution.py
+++ b/solution.py
@@ -2,6 +2,17 @@
 import jax.numpy as jnp
 from jax import lax
 from jax.sharding import PartitionSpec as P
+
+
+def pass_along(x, axis, d):
+    size = lax.axis_size(axis)
+    hops = [(i, (i + 1) % size) for i in range(size)]
+    parts = [x]
+    for reach in range(1, size):
+        parts = [lax.ppermute(parts[0], axis, hops), *parts]
+    out = jnp.concatenate(parts, axis=d)
+    shift = (lax.axis_index(axis) + 1) * parts[-1].shape[d]
+    return jnp.roll(out, shift, axis=d)
 
 
 def shards(left_tiles, right_tile_store, right_index, right_count):
@@ -13,7 +24,7 @@
         jnp.bfloat16
     )
     flat_index = right_index.reshape(-1)
-    shard_rows = lax.all_gather(left_tiles, "col", axis=2, tiled=True)
+    shard_rows = pass_along(left_tiles, "col", 2)
     picked = jnp.take(shard_rows, flat_index, axis=1)
     picked = picked.reshape(
         window_blocks, column_blocks, slot_total, shard_rows.shape[2], shard_rows.shape[3]

time: 107 us -> 142 us (1.33)
  waiting for transfers between devices: 67.3 us -> 87 us
  local copies, waits for them, and re-layouts: 7.65 us -> 22.6 us
    ppermute x0 -> x7, waiting for transfers between devices: none -> 52.9 us  [pass_along(): parts = [lax.ppermute(parts[0], axis, hops), *parts]]
    all_gather x1 -> x0, waiting for transfers between devices: 31.8 us -> none  [shards(): shard_rows = lax.all_gather(left_tiles, 'col', axis=2, tiled=True)]
    unnamed x2 -> x35, local copies, waits for them, and re-layouts: 0.01 us -> 13.6 us
    dynamic_slice x0 -> x1, local copies, waits for them, and re-layouts: none -> 1.49 us  [pass_along(): return jnp.roll(out, shift, axis=d)]
  transfers between devices with their start and end apart: 2 -> 8, of which waited for: 2 -> 8; matrix products, arithmetic and copies ran while one was open for 2% -> 1% of each run, Pallas kernels for 0% -> 0%
where the time goes in v1:
time: 142 us
  waiting for transfers between devices  87 us (61%)
  local copies, waits for them, and re-layouts  22.6 us (16%)
  between operations  13.6 us (10%)
  blocking collectives  8.94 us (6%)
  matrix products  5.95 us (4%)
  other arithmetic  3.06 us (2%)
    ppermute x7, waiting for transfers between devices, pass_along(): parts = [lax.ppermute(parts[0], axis, hops), *parts]  52.9 us
    reduce_scatter x1, waiting for transfers between devices, shards(): lax.psum_scatter(partial_value, 'row', scatter_dimension=2, tiled=True)  34 us
    unnamed x35, local copies, waits for them, and re-layouts  13.6 us
    psum x1, blocking collectives, shards(): column_sums = lax.psum(jnp.sum(squared, axis=(0, 2)), 'row')  8.94 us
    gather x1, local copies, waits for them, and re-layouts, shards(): picked = jnp.take(shard_rows, flat_index, axis=1)  5.98 us
    dot_general x1, matrix products, shards(): jnp.einsum('ajqmb,jqbn->ajmn', picked, right_tile_store, preferred_elemen...  5.95 us
  transfers between devices with their start and end apart: 8, of which 8 were waited for; matrix products, arithmetic and copies ran while one was open for 1% of the time, Pallas kernels for 0%

profile of v1, /device:TPU:0, one launch (start us, length us, event | category | flops | bytes accessed | tf_op | source)
XLA Modules:
  0.0 141.6 jit_solution(1844884422299429673)
XLA Ops:
  7.0 8.3 %collective-permute-done = bf16[2,8,32,256]{3,2,1,0:T(8,128)(2,1)S(1)} collective-permute-done((bf16[2,8,32,256]{3,2,1,0:T(8,128)(2,1)}, bf16[2,8,32,256]{3,2,1,0:T(8,128)(2,1)S(1)}, u32[]{:S(2)}, u32[]{:S(2)}) %collective-permute-start) | collective-permute-done | bytes 262176 | tf_op jit(solution)/shard_map/ppermute | solution.py:12
  16.1 7.6 %collective-permute-done.1 = bf16[2,8,32,256]{3,2,1,0:T(8,128)(2,1)S(1)} collective-permute-done((bf16[2,8,32,256]{3,2,1,0:T(8,128)(2,1)S(1)}, bf16[2,8,32,256]{3,2,1,0:T(8,128)(2,1)S(1)}, u32[]{:S(2)}, u32[]{:S(2)}) %collective-permute-start.1) | collective-permute-done | bytes 262176 | tf_op jit(solution)/shard_map/ppermute | solution.py:12
  24.4 7.6 %collective-permute-done.2 = bf16[2,8,32,256]{3,2,1,0:T(8,128)(2,1)S(1)} collective-permute-done((bf16[2,8,32,256]{3,2,1,0:T(8,128)(2,1)S(1)}, bf16[2,8,32,256]{3,2,1,0:T(8,128)(2,1)S(1)}, u32[]{:S(2)}, u32[]{:S(2)}) %collective-permute-start.2) | collective-permute-done | bytes 262176 | tf_op jit(solution)/shard_map/ppermute | solution.py:12
  32.7 7.6 %collective-permute-done.3 = bf16[2,8,32,256]{3,2,1,0:T(8,128)(2,1)S(1)} collective-permute-done((bf16[2,8,32,256]{3,2,1,0:T(8,128)(2,1)S(1)}, bf16[2,8,32,256]{3,2,1,0:T(8,128)(2,1)S(1)}, u32[]{:S(2)}, u32[]{:S(2)}) %collective-permute-start.3) | collective-permute-done | bytes 262176 | tf_op jit(solution)/shard_map/ppermute | solution.py:12
  41.0 7.7 %collective-permute-done.4 = bf16[2,8,32,256]{3,2,1,0:T(8,128)(2,1)} collective-permute-done((bf16[2,8,32,256]{3,2,1,0:T(8,128)(2,1)S(1)}, bf16[2,8,32,256]{3,2,1,0:T(8,128)(2,1)}, u32[]{:S(2)}, u32[]{:S(2)}) %collective-permute-start.4) | collective-permute-done | bytes 262176 | tf_op jit(solution)/shard_map/ppermute | solution.py:12
  49.4 7.1 %collective-permute-done.5 = bf16[2,8,32,256]{3,2,1,0:T(8,128)(2,1)} collective-permute-done((bf16[2,8,32,256]{3,2,1,0:T(8,128)(2,1)}, bf16[2,8,32,256]{3,2,1,0:T(8,128)(2,1)}, u32[]{:S(2)}, u32[]{:S(2)}) %collective-permute-start.5) | collective-permute-done | bytes 262176 | tf_op jit(solution)/shard_map/ppermute | solution.py:12
  57.5 7.0 %collective-permute-done.6 = bf16[2,8,32,256]{3,2,1,0:T(8,128)(2,1)} collective-permute-done((bf16[2,8,32,256]{3,2,1,0:T(8,128)(2,1)}, bf16[2,8,32,256]{3,2,1,0:T(8,128)(2,1)}, u32[]{:S(2)}, u32[]{:S(2)}) %collective-permute-start.6) | collective-permute-done | bytes 262176 | tf_op jit(solution)/shard_map/ppermute | solution.py:12
  65.5 1.0 constant_dynamic-update-slice_fusion.14
  66.4 1.0 constant_dynamic-update-slice_fusion.13
  67.4 1.0 constant_dynamic-update-slice_fusion.12
  68.4 1.0 constant_dynamic-update-slice_fusion.11
  69.3 1.0 constant_dynamic-update-slice_fusion.10
  70.3 1.0 constant_dynamic-update-slice_fusion.9
  71.3 1.0 constant_dynamic-update-slice_fusion.8
  72.3 1.0 constant_dynamic-update-slice_fusion.7
  73.2 1.0 constant_dynamic-update-slice_fusion.6
  74.2 1.0 constant_dynamic-update-slice_fusion.5
  75.4 1.5 %constant_dynamic-slice_fusion = bf16[2,8,256,256]{3,2,1,0:T(8,128)(2,1)} fusion(bf16[2,8,512,256]{3,2,1,0:T(8,128)(2,1)S(1)} %constant_dynamic-update-slice_fusion, s32[]{:T(128)S(6)} %select_n.37), kind=kLoop, calls=%fused_computation.35 | loop fusion | bytes 4194308 | tf_op jit(solution)/shard_map/jit(_roll_dynamic)/dynamic_slice | solution.py:15
  76.9 6.0 %gather_fusion = bf16[24,2,256,256]{3,2,1,0:T(8,128)(2,1)} fusion(bf16[2,8,256,256]{3,2,1,0:T(8,128)(2,1)} %constant_dynamic-slice_fusion, s32[1024]{0:T(1024)S(1)} %pad_clamp_fusion), kind=kCustom, calls=%fused_computation | custom fusion | bytes 12583008 | tf_op jit(solution)/shard_map/jit(_take)/gather | solution.py:28
  82.8 6.0 %fusion.7 = f32[2,4,256,256]{3,2,0,1:T(8,128)} fusion(bf16[4,6,256,256]{3,2,1,0:T(8,128)(2,1)S(1)} %copy-done, bf16[2,4,6,256,256]{4,3,0,2,1:T(8,128)(2,1)} %bitcast.18, pred[4,6]{1,0:T(4,128)(4,1)S(1)} %get-tuple-element.6, bf16[4,6]{1,0:T(4,128)(2,1)S(1)} %get-tuple-element.5), kind=kOutput, calls=%fused_computation.8 | convolution fusion | flops 1616904192 | bytes 11534408 | tf_op jit(solution)/shard_map/ajqmb,jqbn->ajmn/dot_general | solution.py:33
  88.8 34.0 %reduce-scatter.2.cloned.1.call-done = f32[2,4,64,256]{3,2,0,1:T(8,128)} async-done(((f32[2,4,256,256]{3,2,0,1:T(8,128)}), f32[2,4,64,256]{3,2,0,1:T(8,128)}) %reduce-scatter.2.cloned.1.call-update) | async-done | bytes 524304 | tf_op jit(solution)/shard_map/reduce_scatter | solution.py:36
  122.9 1.1 multiply_reduce_fusion
  124.0 8.9 %psum.7 = f32[4,256]{1,0:T(4,128)S(1)} all-reduce(f32[4,256]{1,0:T(4,128)S(1)} %multiply_reduce_fusion), channel_id=1, replica_groups=mesh['row'=4,'col'=8] {'row'}, use_global_device_ids=true, to_apply=%region_2.3 | all-reduce | flops 1024 | bytes 8192 | tf_op jit(solution)/shard_map/psum | solution.py:38
  132.9 1.1 multiply_convert_fusion
  (41 shorter events, 6.8 us)
Async XLA Ops:
  6.5 76.3 %copy-start = (bf16[4,6,256,256]{3,2,1,0:T(8,128)(2,1)S(1)}, bf16[4,6,256,256]{3,2,1,0:T(8,128)(2,1)}, u32[]{:S(2)}) copy-start(bf16[4,6,256,256]{3,2,1,0:T(8,128)(2,1)} %param.5) | copy-start | bytes 9437188
  6.5 68.8 %copy-start.1 = (bf16[2,8,32,256]{3,2,1,0:T(8,128)(2,1)S(1)}, bf16[2,8,32,256]{3,2,1,0:T(8,128)(2,1)}, u32[]{:S(2)}) copy-start(bf16[2,8,32,256]{3,2,1,0:T(8,128)(2,1)} %param.4) | copy-start | bytes 786436
  6.5 116.3 %reduce-scatter.2.cloned.1.call-start = ((), (), s32[]{:S(2)}) async-start(), calls=%async_computation.1 | async-start | bytes 2621440 | tf_op jit(solution)/shard_map/reduce_scatter | solution.py:36
  6.5 8.8 %collective-permute-start = (bf16[2,8,32,256]{3,2,1,0:T(8,128)(2,1)}, bf16[2,8,32,256]{3,2,1,0:T(8,128)(2,1)S(1)}, u32[]{:S(2)}, u32[]{:S(2)}) collective-permute-start(bf16[2,8,32,256]{3,2,1,0:T(8,128)(2,1)} %param.4), channel_id=1, source_target_pairs={{0,1},{1,2},{2,3},{3,4},{4,5},{5,6},{6,7},{7,0},{8,9},{9,10},{10,1... | collective-permute-start | bytes 786440 | tf_op jit(solution)/shard_map/ppermute | solution.py:12
  15.4 0.7 copy-start.2
  16.1 7.6 %collective-permute-start.1 = (bf16[2,8,32,256]{3,2,1,0:T(8,128)(2,1)S(1)}, bf16[2,8,32,256]{3,2,1,0:T(8,128)(2,1)S(1)}, u32[]{:S(2)}, u32[]{:S(2)}) collective-permute-start(bf16[2,8,32,256]{3,2,1,0:T(8,128)(2,1)S(1)} %collective-permute-done), channel_id=1, source_target_pairs={{0,1},{1,2},{2,3},{3,4},{4,5},{5,6},{6,7},{7,0},{8,9},{9,10},{10,1... | collective-permute-start | bytes 786440 | tf_op jit(solution)/shard_map/ppermute | solution.py:12
  23.7 0.7 copy-start.4
  24.4 7.6 %collective-permute-start.2 = (bf16[2,8,32,256]{3,2,1,0:T(8,128)(2,1)S(1)}, bf16[2,8,32,256]{3,2,1,0:T(8,128)(2,1)S(1)}, u32[]{:S(2)}, u32[]{:S(2)}) collective-permute-start(bf16[2,8,32,256]{3,2,1,0:T(8,128)(2,1)S(1)} %collective-permute-done.1), channel_id=1, source_target_pairs={{0,1},{1,2},{2,3},{3,4},{4,5},{5,6},{6,7},{7,0},{8,9},{9,10},{10,1... | collective-permute-start | bytes 786440 | tf_op jit(solution)/shard_map/ppermute | solution.py:12
  32.0 0.7 copy-start.6
  32.7 7.6 %collective-permute-start.3 = (bf16[2,8,32,256]{3,2,1,0:T(8,128)(2,1)S(1)}, bf16[2,8,32,256]{3,2,1,0:T(8,128)(2,1)S(1)}, u32[]{:S(2)}, u32[]{:S(2)}) collective-permute-start(bf16[2,8,32,256]{3,2,1,0:T(8,128)(2,1)S(1)} %collective-permute-done.2), channel_id=1, source_target_pairs={{0,1},{1,2},{2,3},{3,4},{4,5},{5,6},{6,7},{7,0},{8,9},{9,10},{10,1... | collective-permute-start | bytes 786440 | tf_op jit(solution)/shard_map/ppermute | solution.py:12
  40.3 0.7 copy-start.8
  41.0 7.7 %collective-permute-start.4 = (bf16[2,8,32,256]{3,2,1,0:T(8,128)(2,1)S(1)}, bf16[2,8,32,256]{3,2,1,0:T(8,128)(2,1)}, u32[]{:S(2)}, u32[]{:S(2)}) collective-permute-start(bf16[2,8,32,256]{3,2,1,0:T(8,128)(2,1)S(1)} %collective-permute-done.3), channel_id=1, source_target_pairs={{0,1},{1,2},{2,3},{3,4},{4,5},{5,6},{6,7},{7,0},{8,9},{9,10},{10,1... | collective-permute-start | bytes 786440 | tf_op jit(solution)/shard_map/ppermute | solution.py:12
  48.7 7.9 %collective-permute-start.5 = (bf16[2,8,32,256]{3,2,1,0:T(8,128)(2,1)}, bf16[2,8,32,256]{3,2,1,0:T(8,128)(2,1)}, u32[]{:S(2)}, u32[]{:S(2)}) collective-permute-start(bf16[2,8,32,256]{3,2,1,0:T(8,128)(2,1)} %collective-permute-done.4), channel_id=1, source_target_pairs={{0,1},{1,2},{2,3},{3,4},{4,5},{5,6},{6,7},{7,0},{8,9},{9,10},{10,1... | collective-permute-start | bytes 786440 | tf_op jit(solution)/shard_map/ppermute | solution.py:12
  56.6 7.9 %collective-permute-start.6 = (bf16[2,8,32,256]{3,2,1,0:T(8,128)(2,1)}, bf16[2,8,32,256]{3,2,1,0:T(8,128)(2,1)}, u32[]{:S(2)}, u32[]{:S(2)}) collective-permute-start(bf16[2,8,32,256]{3,2,1,0:T(8,128)(2,1)} %collective-permute-done.5), channel_id=1, source_target_pairs={{0,1},{1,2},{2,3},{3,4},{4,5},{5,6},{6,7},{7,0},{8,9},{9,10},{10,1... | collective-permute-start | bytes 786440 | tf_op jit(solution)/shard_map/ppermute | solution.py:12
  56.6 18.6 %copy-start.9 = (bf16[2,8,32,256]{3,2,1,0:T(8,128)(2,1)S(1)}, bf16[2,8,32,256]{3,2,1,0:T(8,128)(2,1)}, u32[]{:S(2)}) copy-start(bf16[2,8,32,256]{3,2,1,0:T(8,128)(2,1)} %copy-done.8) | copy-start | bytes 786436
  56.6 18.6 %copy-start.7 = (bf16[2,8,32,256]{3,2,1,0:T(8,128)(2,1)S(1)}, bf16[2,8,32,256]{3,2,1,0:T(8,128)(2,1)}, u32[]{:S(2)}) copy-start(bf16[2,8,32,256]{3,2,1,0:T(8,128)(2,1)} %copy-done.6) | copy-start | bytes 786436
  56.6 18.6 %copy-start.5 = (bf16[2,8,32,256]{3,2,1,0:T(8,128)(2,1)S(1)}, bf16[2,8,32,256]{3,2,1,0:T(8,128)(2,1)}, u32[]{:S(2)}) copy-start(bf16[2,8,32,256]{3,2,1,0:T(8,128)(2,1)} %copy-done.4) | copy-start | bytes 786436
  56.6 18.7 %copy-start.3 = (bf16[2,8,32,256]{3,2,1,0:T(8,128)(2,1)S(1)}, bf16[2,8,32,256]{3,2,1,0:T(8,128)(2,1)}, u32[]{:S(2)}) copy-start(bf16[2,8,32,256]{3,2,1,0:T(8,128)(2,1)} %copy-done.2) | copy-start | bytes 786436
Sparse Core Ops, SparseCore 0:
  88.9 33.8 reduce-scatter.1
